TPU v7x, 32 devices: a whole 2x2x4 slice. The times are simulated.
32 devices in a mesh: ccd: 16 (over z, y, x), row: 2 (over core).
Axes of the slice: x: 2, y: 2, z: 4, core: 2. Of those that a mesh axis runs over, the one named last changes fastest.
Arguments:
- exposure: float32 [16, 48, 2048], P('ccd', 'row'), may hold values from -6 to 6
- row_shift: int32 [16], P('ccd'), may hold values from 0 to 7
- row_fraction: bfloat16 [16, 48], P('ccd', 'row'), may hold values from 0 to 1
- column_shift: int32 [16], P('ccd'), may hold values from 0 to 127
- column_fraction: bfloat16 [16, 2048], P('ccd'), may hold values from 0 to 1
- piece_width: int32 [16, 16], P('ccd'), may hold values from 1 to 128
- route_tile: int32 [16, 16], P('ccd'), may hold values from 0 to 15, as said below
- route_cell: int32 [16, 16], P('ccd'), may hold values from 0 to 31, as said below
- template: float32 [16, 48, 4096], P('ccd', 'row'), may hold values from -6 to 6
- match_kernel: bfloat16 [16, 41, 41], P('ccd'), may hold values from -0.15625 to 0.15625
- detection_kernel: bfloat16 [16, 15, 15], P('ccd'), may hold values from -0.375 to 0.375
Outputs:
- difference: float32 [16, 48, 4096], P('ccd', 'row')
- significance: float32 [16, 48, 4096], P('ccd', 'row')
- noise_level: float32 [], replicated
Inputs may be any that keep to these rules, and one draw needn't show every extreme that they name: Piece p of CCD c lands on tile route_tile[c, p]. Every tile receives at least one piece and at most 32 pieces in all; a quarter of the tiles receive exactly 32. No CCD puts more than 2 pieces on one tile, and some CCDs put exactly 2. `route_cell`: pieces that land on one tile fill different cells.
All inputs are finite; a program needn't handle non-finite values.
Results may differ from a plain program's by a relative error of at most 0.0044.
Values may be sent and summed in bfloat16 or wider, within the bound.
A program may use at most 128 MiB of HBM per device.

v0:
```python
import jax
import jax.numpy as jnp
from jax import lax
from jax.sharding import PartitionSpec as P

PW = 128
PAIR = 2
HALO = 8
KS = 41
DK = 15
stack_depth = 5


def extended_2(x, sides, width):
    for axis, dim in sides:
        size, length = (lax.axis_size(axis), x.shape[dim])
        up = [(i, (i + 1) % size) for i in range(size - 1)]
        down = [(j, i) for i, j in up]
        last = lax.slice_in_dim(x, length - width, length, axis=dim)
        first = lax.slice_in_dim(x, 0, width, axis=dim)
        before = lax.ppermute(last, axis, up)
        after = lax.ppermute(first, axis, down)
        x = jnp.concatenate([before, x, after], axis=dim)
    return x


def passed_along(block, axis, distance):
    devices = range(lax.axis_size(axis))
    route = [(i - distance, i) for i in devices if i - distance in devices]
    return lax.ppermute(block, axis, route)


def warp_columns(padded, column_offset, fraction):
    length = fraction.shape[-1]
    leftward = lax.dynamic_slice_in_dim(padded, column_offset, length, 1).astype(jnp.float32)
    rightward = lax.dynamic_slice_in_dim(padded, column_offset + 1, length, 1).astype(jnp.float32)
    weight = fraction.astype(jnp.float32)[None, :]
    return (1.0 - weight) * leftward + weight * rightward


def band_matrix(kernel):
    extent = kernel.shape[0]
    spread = jnp.arange(2 * PW, dtype=jnp.int32)[:, None] - jnp.arange(PW, dtype=jnp.int32)[None, :]
    picker = (spread[:, :, None] == jnp.arange(extent, dtype=jnp.int32)[None, None, :]).astype(
        jnp.bfloat16
    )
    return jnp.einsum("yd,kjd->ykj", kernel, picker, preferred_element_type=jnp.float32).astype(
        jnp.bfloat16
    )


def banded_filter(source, kernel, height):
    extent = kernel.shape[0]
    margin = extent // 2
    blocks_wide = source.shape[1] // PW
    widened = jnp.pad(source, ((0, 0), (margin, 2 * PW - margin)))
    blocked = widened.reshape(widened.shape[0], blocks_wide + 2, PW)
    windows = jnp.concatenate([blocked[:, :blocks_wide], blocked[:, 1 : blocks_wide + 1]], axis=2)
    banded = band_matrix(kernel)
    running = jnp.zeros((height, blocks_wide, PW), jnp.float32)
    for offset in range(0, extent, stack_depth):
        finish = min(offset + stack_depth, extent)
        stacked = jnp.stack(
            [windows[depth_row : depth_row + height] for depth_row in range(offset, finish)], axis=2
        )
        running = running + jnp.einsum(
            "rcgk,gkj->rcj", stacked, banded[offset:finish], preferred_element_type=jnp.float32
        )
    return running.reshape(height, blocks_wide * PW)


def match_template(template, match_kernel, height):
    rounded = template[0].astype(jnp.bfloat16)
    haloed = extended_2(rounded, (("row", 0),), KS // 2)
    return banded_filter(haloed, match_kernel[0], height)


def detection_pass(difference, detection_kernel, height):
    rounded = difference.astype(jnp.bfloat16)
    haloed = extended_2(rounded, (("row", 0),), DK // 2)
    return banded_filter(haloed, detection_kernel[0], height)


def noise_totals(square_sum, live_count):
    return lax.psum((square_sum, live_count), ("ccd", "row"))


def deliver_pieces(
    exposure,
    row_shift,
    row_fraction,
    column_shift,
    column_fraction,
    piece_width,
    route_tile,
    route_cell,
    cell_count,
):
    exposure_band = exposure[0]
    height = exposure_band.shape[0]
    columns = exposure_band.shape[1]
    pieces = columns // PW
    capacity = lax.axis_size("ccd") * PAIR
    below_rows = passed_along(exposure_band[:HALO], "row", -1)
    extended = jnp.concatenate([exposure_band, below_rows], axis=0)
    weight = row_fraction[0].astype(jnp.float32)[:, None]
    upper_rows = lax.dynamic_slice_in_dim(extended, row_shift[0], height, 0)
    lower_rows = lax.dynamic_slice_in_dim(extended, row_shift[0] + 1, height, 0)
    warped_rows = ((1.0 - weight) * upper_rows + weight * lower_rows).astype(jnp.bfloat16)
    padded = jnp.pad(warped_rows, ((0, 0), (0, PW)))
    piece_tile = route_tile[0]
    piece_cell = route_cell[0]
    widths = piece_width[0]
    order_index = jnp.arange(pieces, dtype=jnp.int32)
    earlier = (piece_tile[:, None] == piece_tile[None, :]) & (
        order_index[None, :] < order_index[:, None]
    )
    piece_rank = jnp.sum(earlier.astype(jnp.int32), axis=1)
    target = piece_tile * PAIR + piece_rank
    chooser = jnp.arange(capacity, dtype=jnp.int32)[:, None] == target[None, :]
    chooser_half = chooser.astype(jnp.bfloat16)
    sent_cell = jnp.sum(jnp.where(chooser, piece_cell[None, :] + 1, 0), axis=1) - 1
    sent_width = jnp.sum(jnp.where(chooser, widths[None, :], 0), axis=1)
    lane_index = jnp.arange(PW, dtype=jnp.int32)
    warped = warp_columns(padded, column_shift[0], column_fraction[0]).astype(jnp.bfloat16)
    keep_mask = (lane_index[None, :] < widths[:, None]).reshape(columns)
    warped = jnp.where(keep_mask[None, :], warped, jnp.zeros((), jnp.bfloat16))
    outgoing = jnp.einsum(
        "sp,rpj->srj",
        chooser_half,
        warped.reshape(height, pieces, PW),
        preferred_element_type=jnp.float32,
    ).astype(jnp.bfloat16)
    incoming, got_cell, got_width = (
        lax.all_to_all(outgoing, "ccd", split_axis=0, concat_axis=0, tiled=True),
        lax.all_to_all(sent_cell, "ccd", split_axis=0, concat_axis=0, tiled=True),
        lax.all_to_all(sent_width, "ccd", split_axis=0, concat_axis=0, tiled=True),
    )
    placer = jnp.arange(cell_count, dtype=jnp.int32)[:, None] == got_cell[None, :]
    science = jnp.einsum(
        "qs,srj->rqj", placer.astype(jnp.bfloat16), incoming, preferred_element_type=jnp.float32
    ).reshape(height, cell_count * PW)
    cell_width = jnp.sum(jnp.where(placer, got_width[None, :], 0), axis=1).astype(jnp.int32)
    live_mask = (lane_index[None, :] < cell_width[:, None]).reshape(cell_count * PW)
    return (science, live_mask, cell_width)


def on_device(
    exposure,
    row_shift,
    row_fraction,
    column_shift,
    column_fraction,
    piece_width,
    route_tile,
    route_cell,
    template,
    match_kernel,
    detection_kernel,
):
    height = exposure.shape[1]
    cell_count = template.shape[2] // PW
    science, live_mask, cell_width = deliver_pieces(
        exposure,
        row_shift,
        row_fraction,
        column_shift,
        column_fraction,
        piece_width,
        route_tile,
        route_cell,
        cell_count,
    )
    matched = match_template(template, match_kernel, height)
    difference = jnp.where(live_mask[None, :], science - matched, jnp.zeros((), jnp.float32))
    square_sum = jnp.sum(difference * difference)
    live_count = (height * jnp.sum(cell_width)).astype(jnp.float32)
    filtered = detection_pass(difference, detection_kernel, height)
    total_square, total_count = noise_totals(square_sum, live_count)
    noise_level = total_square / total_count
    detect_weights = detection_kernel[0].astype(jnp.float32)
    kernel_norm = jnp.sum(detect_weights * detect_weights)
    significance = filtered / jnp.sqrt(1.0 + noise_level * kernel_norm)
    return (difference[None], significance[None], noise_level)


def solution(mesh):
    return jax.shard_map(
        on_device,
        mesh=mesh,
        in_specs=(
            P("ccd", "row", None),
            P("ccd"),
            P("ccd", "row"),
            P("ccd"),
            P("ccd", None),
            P("ccd", None),
            P("ccd", None),
            P("ccd", None),
            P("ccd", "row", None),
            P("ccd", None, None),
            P("ccd", None, None),
        ),
        out_specs=(P("ccd", "row", None), P("ccd", "row", None), P()),
        check_vma=False,
    )
```

profile of v0, /device:TPU:0, one launch (start us, length us, event | category | flops | bytes accessed | tf_op | source)
XLA Modules:
  0.0 126.3 jit_solution(17106949905012191423)
XLA Ops:
  0.6 1.0 convert_element_type.82
  1.7 0.8 slice_bitcast_fusion.10
  2.5 3.1 %collective-permute-start.1 = (bf16[20,4096]{1,0:T(8,128)(2,1)}, bf16[20,4096]{1,0:T(8,128)(2,1)}, u32[]{:S(2)}, u32[]{:S(2)}) collective-permute-start(bf16[20,4096]{1,0:T(8,128)(2,1)} %get-tuple-element.53), channel_id=1, source_target_pairs={{0,1},{2,3},{4,5},{6,7},{8,9},{10,11},{12,13},{14,15},{16,17},{18,... | collective-permute-start | bytes 491528 | tf_op jit(solution)/shard_map/ppermute | solution.py:21
  5.5 1.3 %collective-permute-start.2 = (bf16[20,4096]{1,0:T(8,128)(2,1)}, bf16[20,4096]{1,0:T(8,128)(2,1)}, u32[]{:S(2)}, u32[]{:S(2)}) collective-permute-start(bf16[20,4096]{1,0:T(8,128)(2,1)} %get-tuple-element.54), channel_id=1, source_target_pairs={{1,0},{3,2},{5,4},{7,6},{9,8},{11,10},{13,12},{15,14},{17,16},{19,... | collective-permute-start | bytes 491528 | tf_op jit(solution)/shard_map/ppermute | solution.py:22
  6.8 1.5 %slice_bitcast_fusion.11 = f32[8,2048]{1,0:T(8,128)} fusion(f32[1,24,2048]{2,1,0:T(8,128)} %param.11), kind=kLoop, calls=%fused_computation.369 | loop fusion | bytes 131072 | tf_op jit(solution)/shard_map/slice | solution.py:104
  8.3 1.3 %collective-permute-start = (f32[8,2048]{1,0:T(8,128)}, f32[8,2048]{1,0:T(8,128)}, u32[]{:S(2)}, u32[]{:S(2)}) collective-permute-start(f32[8,2048]{1,0:T(8,128)} %slice_bitcast_fusion.11), channel_id=1, source_target_pairs={{1,0},{3,2},{5,4},{7,6},{9,8},{11,10},{13,12},{15,14},{17,16},{19,... | collective-permute-start | bytes 196616 | tf_op jit(solution)/shard_map/ppermute | solution.py:30
  9.6 0.9 convert_reduce_fusion
  10.5 0.7 fusion.228
  11.2 0.6 copy-done.12
  11.7 1.3 select_reduce_fusion.2
  13.0 0.7 sub.70
  13.7 7.7 %all-to-all-start = ((s32[16,2,1]{1,2,0:T(1,128)}), s32[16,2,1]{1,2,0:T(1,128)}, u32[]{:S(2)}, u32[]{:S(2)}) async-start(s32[16,2,1]{1,2,0:T(1,128)} %bitcast.4), calls=%async_computation | async-start | bytes 16384 | tf_op jit(solution)/shard_map/all_to_all | solution.py:136
  21.4 1.0 convert_bitcast_fusion.1
  22.5 1.6 %convert_bitcast_fusion = bf16[41,256,128]{2,0,1:T(8,128)(2,1)S(1)} fusion(s32[256,128]{1,0:T(8,128)S(1)} %iota_subtract_fusion, bf16[1,41,41]{2,1,0:T(8,128)(2,1)S(1)} %copy-done), kind=kOutput, calls=%fused_computation.83 | convolution fusion | flops 112852992 | bytes 2821410 | tf_op jit(solution)/shard_map/yd,kjd->ykj/dot_general | solution.py:47
  24.1 2.2 %fusion.231 = (bf16[5,256,128]{2,0,1:T(8,128)(2,1)S(1)}, bf16[5,256,128,1]{2,0,1,3:T(8,128)(2,1)}, bf16[5,256,128,1]{2,0,1,3:T(8,128)(2,1)}, bf16[5,256,128,1]{2...) fusion(bf16[41,256,128]{2,0,1:T(8,128)(2,1)S(1)} %convert_bitca, ...), kind=kLoop, calls=%fused_computation.398 | loop fusion | bytes 5242880 | tf_op jit(solution)/shard_map/slice | solution.py:67
  26.3 0.7 slice.412
  27.0 0.6 bitcast_convert_fusion
  27.6 0.6 broadcast_subtract_fusion.1
  28.2 0.6 fusion.225
  28.9 0.6 broadcast_subtract_fusion
  29.5 0.6 convert_element_type.74
  30.1 0.7 multiply_reduce_fusion.1
  30.7 0.6 fusion.4
  32.7 1.3 %all_to_all.14 = s32[16,2,1]{1,0,2:T(8,128)} reshape(s32[32]{0:T(128)} %get-tuple-element.5) | data formatting | bytes 256 | tf_op jit(solution)/shard_map/all_to_all | solution.py:137
  34.0 1.3 %fusion.232 = (bf16[5,256,128]{2,0,1:T(8,128)(2,1)}, bf16[5,256,128,1]{2,0,1,3:T(8,128)(2,1)}, bf16[5,256,128,1]{2,0,1,3:T(8,128)(2,1)}) fusion(bf16[15,256,128]{2,0,1:T(8,128)(2,1)S(1)} %fusion.4), kind=kLoop, calls=%fused_computation.399 | loop fusion | bytes 1966080 | tf_op jit(solution)/shard_map/slice | solution.py:67
  35.3 6.9 %all-to-all-start.1 = ((s32[16,2,1]{1,2,0:T(1,128)}), s32[16,2,1]{1,2,0:T(1,128)S(1)}, u32[]{:S(2)}, u32[]{:S(2)}) async-start(s32[16,2,1]{1,2,0:T(1,128)} %bitcast.401), calls=%async_computation.1 | async-start | bytes 16384 | tf_op jit(solution)/shard_map/all_to_all | solution.py:137
  42.2 0.5 broadcast.128
  42.7 1.4 %reduce.8 = s32[16,2]{1,0:T(8,128)S(1)} reduce(s32[16,2,1]{1,2,0:T(1,128)} %all-to-all-done, s32[]{:T(128)} %broadcast.128), dimensions={2}, to_apply=%all_to_all.13.reduce_sub_computation.3 | reduce | bytes 260 | tf_op jit(solution)/shard_map/all_to_all | solution.py:136
  44.2 5.3 %all-to-all-done.1 = s32[16,2,1]{1,2,0:T(1,128)S(1)} async-done(((s32[16,2,1]{1,2,0:T(1,128)}), s32[16,2,1]{1,2,0:T(1,128)S(1)}, u32[]{:S(2)}, u32[]{:S(2)}) %all-to-all-start.1) | async-done | bytes 160 | tf_op jit(solution)/shard_map/all_to_all | solution.py:137
  49.5 0.7 reduce.9
  50.3 0.6 select_reduce_fusion
  51.7 1.1 fusion.210
  52.7 0.8 fusion.215
  53.6 1.0 convolution_convert_fusion
  54.6 0.8 copy.95
  55.4 4.4 %all-to-all-start.2 = ((bf16[32,24,128]{2,1,0:T(8,128)(2,1)}), bf16[32,24,128]{2,1,0:T(8,128)(2,1)}, u32[]{:S(2)}, u32[]{:S(2)}) async-start(bf16[32,24,128]{2,1,0:T(8,128)(2,1)} %copy.95), calls=%async_computation.2 | async-start | bytes 393216 | tf_op jit(solution)/shard_map/all_to_all | solution.py:135
  59.7 1.3 %fusion.23 = bf16[64,4352]{1,0:T(8,128)(2,1)S(1)} fusion(bf16[20,4096]{1,0:T(8,128)(2,1)} %collective-permute-done.2, bf16[24,4096]{1,0:T(8,128)(2,1)S(1)} %convert_bitcast_fusion.1, bf16[20,4096]{1,0:T(8,128)(2,1)} %collective-permute-done.1), kind=kLoop, calls=%fused_computation.153 | loop fusion | flops 3342336 | bytes 1081344 | tf_op jit(solution)/shard_map/concatenate | solution.py:23
  61.0 0.3 reshape.169
  61.9 0.4 fusion.98
  62.4 0.3 fusion.113
  62.8 0.3 fusion.128
  63.8 0.7 copy-done.4
  64.5 0.7 convolution_bitcast_fusion.3
  65.1 0.7 convolution_bitcast_fusion.4
  65.8 0.3 copy-done.2
  66.2 0.7 convolution_bitcast_fusion.5
  66.9 0.7 convolution_bitcast_fusion.6
  67.6 0.7 convolution_bitcast_fusion.7
  68.3 0.7 convolution_bitcast_fusion.8
  69.0 0.7 convolution_bitcast_fusion.9
  69.6 0.8 fusion.12
  70.5 0.3 convolution_add_fusion
  70.8 1.8 %multiply_reduce_fusion = (f32[]{:T(128)}, f32[24,32,128]{2,1,0:T(8,128)S(1)}) fusion(pred[32,128]{1,0:T(8,128)(4,1)S(1)} %get-tuple-element.55, f32[24,32,128]{2,1,0:T(8,128)S(1)} %convolution_add_fusion, s32[32]{0:T(128)S(1)} %eq.80, bf16[32,24,128]{2,1,0:T(8,128)(2,1)} %all-to-all-done.2), kind=kOutput, calls=%fused_computation.333 | convolution fusion | flops 6685695 | bytes 987268 | tf_op jit(solution)/shard_map/qs,srj->rqj/dot_general | solution.py:140
  72.7 0.2 fusion.189
  72.9 2.3 %collective-permute-start.3 = (bf16[7,4096]{1,0:T(8,128)(2,1)S(1)}, bf16[7,4096]{1,0:T(8,128)(2,1)S(1)}, u32[]{:S(2)}, u32[]{:S(2)}) collective-permute-start(bf16[7,4096]{1,0:T(8,128)(2,1)S(1)} %get-tuple-element.51), channel_id=1, source_target_pairs={{0,1},{2,3},{4,5},{6,7},{8,9},{10,11},{12,13},{14,15},{16,17},{18,... | collective-permute-start | bytes 172040 | tf_op jit(solution)/shard_map/ppermute | solution.py:21
  75.3 1.3 %collective-permute-start.4 = (bf16[7,4096]{1,0:T(8,128)(2,1)S(1)}, bf16[7,4096]{1,0:T(8,128)(2,1)S(1)}, u32[]{:S(2)}, u32[]{:S(2)}) collective-permute-start(bf16[7,4096]{1,0:T(8,128)(2,1)S(1)} %get-tuple-element.52), channel_id=1, source_target_pairs={{1,0},{3,2},{5,4},{7,6},{9,8},{11,10},{13,12},{15,14},{17,16},{19,... | collective-permute-start | bytes 172040 | tf_op jit(solution)/shard_map/ppermute | solution.py:22
  76.6 0.8 broadcast_select_fusion
  77.4 40.2 %all-reduce.3 = (f32[]{:T(128)}, f32[]{:T(128)}) all-reduce(f32[]{:T(128)} %get-tuple-element.57, f32[]{:T(128)S(6)} %convert_element_type.89), channel_id=1, replica_groups=mesh['ccd'=16,'row'=2] {'ccd','row'}, use_global_device_ids=true, to_apply=%region_5.6 | all-reduce | flops 2 | bytes 16 | tf_op jit(solution)/shard_map/psum | solution.py:85
  121.1 0.8 copy-done.6
  121.9 0.7 convolution_bitcast_fusion
  122.6 0.7 convolution_bitcast_fusion.1
  123.3 0.3 copy-done.7
  123.7 0.7 fusion.15
  124.4 0.8 div.22
  (75 shorter events, 3.3 us)
Async XLA Ops:
  0.6 21.8 %copy-start = (bf16[1,41,41]{2,1,0:T(8,128)(2,1)S(1)}, bf16[1,41,41]{2,1,0:T(8,128)(2,1)}, u32[]{:S(2)}) copy-start(bf16[1,41,41]{2,1,0:T(8,128)(2,1)} %param.20) | copy-start | bytes 10090
  2.5 57.3 %collective-permute-start.1 = (bf16[20,4096]{1,0:T(8,128)(2,1)}, bf16[20,4096]{1,0:T(8,128)(2,1)}, u32[]{:S(2)}, u32[]{:S(2)}) collective-permute-start(bf16[20,4096]{1,0:T(8,128)(2,1)} %get-tuple-element.53), channel_id=1, source_target_pairs={{0,1},{2,3},{4,5},{6,7},{8,9},{10,11},{12,13},{14,15},{16,17},{18,... | collective-permute-start | bytes 491528 | tf_op jit(solution)/shard_map/ppermute | solution.py:21
  5.5 54.2 %collective-permute-start.2 = (bf16[20,4096]{1,0:T(8,128)(2,1)}, bf16[20,4096]{1,0:T(8,128)(2,1)}, u32[]{:S(2)}, u32[]{:S(2)}) collective-permute-start(bf16[20,4096]{1,0:T(8,128)(2,1)} %get-tuple-element.54), channel_id=1, source_target_pairs={{1,0},{3,2},{5,4},{7,6},{9,8},{11,10},{13,12},{15,14},{17,16},{19,... | collective-permute-start | bytes 491528 | tf_op jit(solution)/shard_map/ppermute | solution.py:22
  8.3 43.4 %collective-permute-start = (f32[8,2048]{1,0:T(8,128)}, f32[8,2048]{1,0:T(8,128)}, u32[]{:S(2)}, u32[]{:S(2)}) collective-permute-start(f32[8,2048]{1,0:T(8,128)} %slice_bitcast_fusion.11), channel_id=1, source_target_pairs={{1,0},{3,2},{5,4},{7,6},{9,8},{11,10},{13,12},{15,14},{17,16},{19,... | collective-permute-start | bytes 196616 | tf_op jit(solution)/shard_map/ppermute | solution.py:30
  11.2 0.6 copy-start.12
  13.7 21.7 %all-to-all-start = ((s32[16,2,1]{1,2,0:T(1,128)}), s32[16,2,1]{1,2,0:T(1,128)}, u32[]{:S(2)}, u32[]{:S(2)}) async-start(s32[16,2,1]{1,2,0:T(1,128)} %bitcast.4), calls=%async_computation | async-start | bytes 16384 | tf_op jit(solution)/shard_map/all_to_all | solution.py:136
  24.0 3.0 %copy-start.14 = (bf16[1,24]{1,0:T(2,128)(2,1)S(1)}, bf16[1,24]{1,0:T(2,128)(2,1)}, u32[]{:S(2)}) copy-start(bf16[1,24]{1,0:T(2,128)(2,1)} %param.13) | copy-start | bytes 148
  24.1 4.2 %copy-start.13 = (s32[1,16]{1,0:T(1,128)S(1)}, s32[1,16]{1,0:T(1,128)}, u32[]{:S(2)}) copy-start(s32[1,16]{1,0:T(1,128)} %param.16) | copy-start | bytes 196
  24.1 4.8 %copy-start.10 = (bf16[1,2048]{1,0:T(2,128)(2,1)S(1)}, bf16[1,2048]{1,0:T(2,128)(2,1)}, u32[]{:S(2)}) copy-start(bf16[1,2048]{1,0:T(2,128)(2,1)} %param.15) | copy-start | bytes 12292
  24.1 6.0 %copy-start.11 = (bf16[1,15,15]{2,1,0:T(8,128)(2,1)S(1)}, bf16[1,15,15]{2,1,0:T(8,128)(2,1)}, u32[]{:S(2)}) copy-start(bf16[1,15,15]{2,1,0:T(8,128)(2,1)} %param.21) | copy-start | bytes 1354
  30.7 20.9 %copy-start.8 = (f32[1,24,2048]{2,1,0:T(8,128)S(1)}, f32[1,24,2048]{2,1,0:T(8,128)}, u32[]{:S(2)}) copy-start(f32[1,24,2048]{2,1,0:T(8,128)} %param.11) | copy-start | bytes 589828
  35.3 14.2 %all-to-all-start.1 = ((s32[16,2,1]{1,2,0:T(1,128)}), s32[16,2,1]{1,2,0:T(1,128)S(1)}, u32[]{:S(2)}, u32[]{:S(2)}) async-start(s32[16,2,1]{1,2,0:T(1,128)} %bitcast.401), calls=%async_computation.1 | async-start | bytes 16384 | tf_op jit(solution)/shard_map/all_to_all | solution.py:137
  55.4 15.5 %all-to-all-start.2 = ((bf16[32,24,128]{2,1,0:T(8,128)(2,1)}), bf16[32,24,128]{2,1,0:T(8,128)(2,1)}, u32[]{:S(2)}, u32[]{:S(2)}) async-start(bf16[32,24,128]{2,1,0:T(8,128)(2,1)} %copy.95), calls=%async_computation.2 | async-start | bytes 393216 | tf_op jit(solution)/shard_map/all_to_all | solution.py:135
  63.4 1.0 copy-start.4
  63.6 1.5 %copy-start.3 = (bf16[5,256,128,1]{2,0,1,3:T(8,128)(2,1)S(1)}, bf16[5,256,128,1]{2,0,1,3:T(8,128)(2,1)}, u32[]{:S(2)}) copy-start(bf16[5,256,128,1]{2,0,1,3:T(8,128)(2,1)} %get-tuple-element.11) | copy-start | bytes 983044
  65.1 1.0 copy-start.2
  65.8 1.1 copy-start.1
  69.6 0.9 copy-start.9
  72.9 46.7 %collective-permute-start.3 = (bf16[7,4096]{1,0:T(8,128)(2,1)S(1)}, bf16[7,4096]{1,0:T(8,128)(2,1)S(1)}, u32[]{:S(2)}, u32[]{:S(2)}) collective-permute-start(bf16[7,4096]{1,0:T(8,128)(2,1)S(1)} %get-tuple-element.51), channel_id=1, source_target_pairs={{0,1},{2,3},{4,5},{6,7},{8,9},{10,11},{12,13},{14,15},{16,17},{18,... | collective-permute-start | bytes 172040 | tf_op jit(solution)/shard_map/ppermute | solution.py:21
  75.3 44.3 %collective-permute-start.4 = (bf16[7,4096]{1,0:T(8,128)(2,1)S(1)}, bf16[7,4096]{1,0:T(8,128)(2,1)S(1)}, u32[]{:S(2)}, u32[]{:S(2)}) collective-permute-start(bf16[7,4096]{1,0:T(8,128)(2,1)S(1)} %get-tuple-element.52), channel_id=1, source_target_pairs={{1,0},{3,2},{5,4},{7,6},{9,8},{11,10},{13,12},{15,14},{17,16},{19,... | collective-permute-start | bytes 172040 | tf_op jit(solution)/shard_map/ppermute | solution.py:22
  120.9 1.1 copy-start.6
  121.1 1.6 %copy-start.5 = (bf16[5,256,128,1]{2,0,1,3:T(8,128)(2,1)S(1)}, bf16[5,256,128,1]{2,0,1,3:T(8,128)(2,1)}, u32[]{:S(2)}) copy-start(bf16[5,256,128,1]{2,0,1,3:T(8,128)(2,1)} %get-tuple-element.19) | copy-start | bytes 983044
  122.6 1.0 copy-start.7
where the time goes:
time: 127 us; the launch traced here: 126 us
  blocking collectives  40.2 us (32%)
  starting transfers between devices  28.2 us (22%)
  other arithmetic  18.6 us (15%)
  local copies, waits for them, and re-layouts  14.7 us (12%)
  matrix products  12.8 us (10%)
  between operations  6.44 us (5%)
  waiting for transfers between devices  5.34 us (4%)
    psum x1, blocking collectives, noise_totals(): return lax.psum((square_sum, live_count), ('ccd', 'row'))  40.2 us
    dot_general x12, matrix products, banded_filter(): jnp.einsum('rcgk,gkj->rcj', stacked, banded[offset:finish], preferred_ele...  7.79 us
    all_to_all x1, starting transfers between devices, deliver_pieces(): lax.all_to_all(sent_cell, 'ccd', split_axis=0, concat_axis=0, tiled=True)  7.73 us
    all_to_all x1, starting transfers between devices, deliver_pieces(): lax.all_to_all(sent_width, 'ccd', split_axis=0, concat_axis=0, tiled=True)  6.86 us
    ppermute x2, starting transfers between devices, extended_2(): before = lax.ppermute(last, axis, up)  5.4 us
    all_to_all x1, waiting for transfers between devices, deliver_pieces(): lax.all_to_all(sent_width, 'ccd', split_axis=0, concat_axis=0, tiled=True)  5.33 us
    all_to_all x1, starting transfers between devices, deliver_pieces(): lax.all_to_all(outgoing, 'ccd', split_axis=0, concat_axis=0, tiled=True)  4.35 us
    slice x3, local copies, waits for them, and re-layouts, banded_filter(): banded[offset:finish]  4.24 us
  transfers between devices with their start and end apart: 8, of which 1 were waited for; matrix products, arithmetic and copies ran while one was open for 27% of the time, Pallas kernels for 0%

commit v1 on v0

--- a/solution.py
+++ b/solution.py
@@ -82,7 +82,7 @@
 
 
 def noise_totals(square_sum, live_count):
-    return lax.psum((square_sum, live_count), ("ccd", "row"))
+    return lax.psum(lax.psum((square_sum, live_count), "row"), "ccd")
 
 
 def deliver_pieces(

time: 127 us -> 133 us (1.047)
  blocking collectives: 40.2 us -> 46 us
    psum x1 -> x2, blocking collectives: 40.2 us -> 46 us  [noise_totals(): return lax.psum(lax.psum((square_sum, live_count), 'row'), 'ccd')]
  transfers between devices with their start and end apart: 8 -> 8, of which waited for: 1 -> 1; matrix products, arithmetic and copies ran while one was open for 27% -> 25% of each run, Pallas kernels for 0% -> 0%
where the time goes in v1:
time: 133 us; the launch traced here: 132 us
  blocking collectives  46 us (35%)
  starting transfers between devices  28.2 us (21%)
  other arithmetic  18.5 us (14%)
  local copies, waits for them, and re-layouts  14.7 us (11%)
  matrix products  12.7 us (10%)
  between operations  6.43 us (5%)
  waiting for transfers between devices  5.33 us (4%)
    psum x2, blocking collectives, noise_totals(): return lax.psum(lax.psum((square_sum, live_count), 'row'), 'ccd')  46 us
    dot_general x12, matrix products, banded_filter(): jnp.einsum('rcgk,gkj->rcj', stacked, banded[offset:finish], preferred_ele...  7.78 us
    all_to_all x1, starting transfers between devices, deliver_pieces(): lax.all_to_all(sent_cell, 'ccd', split_axis=0, concat_axis=0, tiled=True)  7.73 us
    all_to_all x1, starting transfers between devices, deliver_pieces(): lax.all_to_all(sent_width, 'ccd', split_axis=0, concat_axis=0, tiled=True)  6.85 us
    ppermute x2, starting transfers between devices, extended_2(): before = lax.ppermute(last, axis, up)  5.39 us
    all_to_all x1, waiting for transfers between devices, deliver_pieces(): lax.all_to_all(sent_width, 'ccd', split_axis=0, concat_axis=0, tiled=True)  5.32 us
    all_to_all x1, starting transfers between devices, deliver_pieces(): lax.all_to_all(outgoing, 'ccd', split_axis=0, concat_axis=0, tiled=True)  4.35 us
    slice x3, local copies, waits for them, and re-layouts, banded_filter(): banded[offset:finish]  4.23 us
  transfers between devices with their start and end apart: 8, of which 1 were waited for; matrix products, arithmetic and copies ran while one was open for 25% of the time, Pallas kernels for 0%

profile of v1, /device:TPU:0, one launch (start us, length us, event | category | flops | bytes accessed | tf_op | source)
XLA Modules:
  0.0 131.8 jit_solution(885794268401327708)
XLA Ops:
  0.6 1.0 convert_element_type.82
  1.7 0.8 slice_bitcast_fusion.10
  2.5 3.1 %collective-permute-start.1 = (bf16[20,4096]{1,0:T(8,128)(2,1)}, bf16[20,4096]{1,0:T(8,128)(2,1)}, u32[]{:S(2)}, u32[]{:S(2)}) collective-permute-start(bf16[20,4096]{1,0:T(8,128)(2,1)} %get-tuple-element.55), channel_id=1, source_target_pairs={{0,1},{2,3},{4,5},{6,7},{8,9},{10,11},{12,13},{14,15},{16,17},{18,... | collective-permute-start | bytes 491528 | tf_op jit(solution)/shard_map/ppermute | solution.py:21
  5.5 1.3 collective-permute-start.2
  6.8 1.5 %slice_bitcast_fusion.11 = f32[8,2048]{1,0:T(8,128)} fusion(f32[1,24,2048]{2,1,0:T(8,128)} %param.11), kind=kLoop, calls=%fused_computation.369 | loop fusion | bytes 131072 | tf_op jit(solution)/shard_map/slice | solution.py:104
  8.3 1.3 collective-permute-start
  9.6 0.9 convert_reduce_fusion
  10.5 0.7 fusion.228
  11.2 0.5 copy-done.12
  11.7 1.3 select_reduce_fusion.2
  12.9 0.7 sub.70
  13.6 7.7 %all-to-all-start = ((s32[16,2,1]{1,2,0:T(1,128)}), s32[16,2,1]{1,2,0:T(1,128)}, u32[]{:S(2)}, u32[]{:S(2)}) async-start(s32[16,2,1]{1,2,0:T(1,128)} %bitcast.4), calls=%async_computation | async-start | bytes 16384 | tf_op jit(solution)/shard_map/all_to_all | solution.py:136
  21.4 1.0 convert_bitcast_fusion.1
  22.4 1.6 %convert_bitcast_fusion = bf16[41,256,128]{2,0,1:T(8,128)(2,1)S(1)} fusion(s32[256,128]{1,0:T(8,128)S(1)} %iota_subtract_fusion, bf16[1,41,41]{2,1,0:T(8,128)(2,1)S(1)} %copy-done), kind=kOutput, calls=%fused_computation.83 | convolution fusion | flops 112852992 | bytes 2821410 | tf_op jit(solution)/shard_map/yd,kjd->ykj/dot_general | solution.py:47
  24.0 2.2 %fusion.231 = (bf16[5,256,128]{2,0,1:T(8,128)(2,1)S(1)}, bf16[5,256,128,1]{2,0,1,3:T(8,128)(2,1)}, bf16[5,256,128,1]{2,0,1,3:T(8,128)(2,1)}, bf16[5,256,128,1]{2...) fusion(bf16[41,256,128]{2,0,1:T(8,128)(2,1)S(1)} %convert_bitca, ...), kind=kLoop, calls=%fused_computation.398 | loop fusion | bytes 5242880 | tf_op jit(solution)/shard_map/slice | solution.py:67
  26.3 0.7 slice.412
  27.0 0.5 bitcast_convert_fusion
  27.5 0.6 broadcast_subtract_fusion.1
  28.1 0.6 fusion.225
  28.8 0.6 broadcast_subtract_fusion
  29.4 0.6 convert_element_type.74
  30.0 0.6 multiply_reduce_fusion.1
  30.6 0.6 fusion.4
  32.5 1.3 %all_to_all.14 = s32[16,2,1]{1,0,2:T(8,128)} reshape(s32[32]{0:T(128)} %get-tuple-element.5) | data formatting | bytes 256 | tf_op jit(solution)/shard_map/all_to_all | solution.py:137
  33.9 1.3 fusion.232
  35.2 6.9 %all-to-all-start.1 = ((s32[16,2,1]{1,2,0:T(1,128)}), s32[16,2,1]{1,2,0:T(1,128)S(1)}, u32[]{:S(2)}, u32[]{:S(2)}) async-start(s32[16,2,1]{1,2,0:T(1,128)} %bitcast.401), calls=%async_computation.1 | async-start | bytes 16384 | tf_op jit(solution)/shard_map/all_to_all | solution.py:137
  42.0 0.5 broadcast.128
  42.5 1.4 %reduce.8 = s32[16,2]{1,0:T(8,128)S(1)} reduce(s32[16,2,1]{1,2,0:T(1,128)} %all-to-all-done, s32[]{:T(128)} %broadcast.128), dimensions={2}, to_apply=%all_to_all.13.reduce_sub_computation.3 | reduce | bytes 260 | tf_op jit(solution)/shard_map/all_to_all | solution.py:136
  44.0 5.3 %all-to-all-done.1 = s32[16,2,1]{1,2,0:T(1,128)S(1)} async-done(((s32[16,2,1]{1,2,0:T(1,128)}), s32[16,2,1]{1,2,0:T(1,128)S(1)}, u32[]{:S(2)}, u32[]{:S(2)}) %all-to-all-start.1) | async-done | bytes 160 | tf_op jit(solution)/shard_map/all_to_all | solution.py:137
  49.3 0.7 reduce.9
  50.1 0.6 select_reduce_fusion
  51.5 1.1 fusion.210
  52.5 0.8 fusion.215
  53.4 0.9 convolution_convert_fusion
  54.3 0.8 copy.95
  55.1 4.4 %all-to-all-start.2 = ((bf16[32,24,128]{2,1,0:T(8,128)(2,1)}), bf16[32,24,128]{2,1,0:T(8,128)(2,1)}, u32[]{:S(2)}, u32[]{:S(2)}) async-start(bf16[32,24,128]{2,1,0:T(8,128)(2,1)} %copy.95), calls=%async_computation.2 | async-start | bytes 393216 | tf_op jit(solution)/shard_map/all_to_all | solution.py:135
  59.5 1.3 fusion.23
  60.8 0.3 reshape.169
  61.6 0.4 fusion.98
  62.2 0.3 fusion.113
  62.6 0.3 fusion.128
  63.5 0.7 copy-done.4
  64.2 0.7 convolution_bitcast_fusion.3
  64.9 0.7 convolution_bitcast_fusion.4
  65.6 0.3 copy-done.2
  65.9 0.7 convolution_bitcast_fusion.5
  66.7 0.7 convolution_bitcast_fusion.6
  67.3 0.7 convolution_bitcast_fusion.7
  68.0 0.7 convolution_bitcast_fusion.8
  68.7 0.7 convolution_bitcast_fusion.9
  69.4 0.8 fusion.12
  70.3 0.3 convolution_add_fusion
  70.6 1.8 %multiply_reduce_fusion = (f32[]{:T(128)}, f32[24,32,128]{2,1,0:T(8,128)S(1)}) fusion(pred[32,128]{1,0:T(8,128)(4,1)S(1)} %get-tuple-element.57, f32[24,32,128]{2,1,0:T(8,128)S(1)} %convolution_add_fusion, s32[32]{0:T(128)S(1)} %eq.80, bf16[32,24,128]{2,1,0:T(8,128)(2,1)} %all-to-all-done.2), kind=kOutput, calls=%fused_computation.333 | convolution fusion | flops 6685695 | bytes 987268 | tf_op jit(solution)/shard_map/qs,srj->rqj/dot_general | solution.py:140
  72.7 2.3 %collective-permute-start.3 = (bf16[7,4096]{1,0:T(8,128)(2,1)S(1)}, bf16[7,4096]{1,0:T(8,128)(2,1)S(1)}, u32[]{:S(2)}, u32[]{:S(2)}) collective-permute-start(bf16[7,4096]{1,0:T(8,128)(2,1)S(1)} %get-tuple-element.53), channel_id=1, source_target_pairs={{0,1},{2,3},{4,5},{6,7},{8,9},{10,11},{12,13},{14,15},{16,17},{18,... | collective-permute-start | bytes 172040 | tf_op jit(solution)/shard_map/ppermute | solution.py:21
  75.0 1.3 collective-permute-start.4
  76.3 0.8 broadcast_select_fusion
  77.1 3.9 %all-reduce.4 = (f32[]{:T(128)}, f32[]{:T(128)}) all-reduce(f32[]{:T(128)} %get-tuple-element.59, f32[]{:T(128)S(6)} %convert_element_type.89), channel_id=1, replica_groups=mesh['ccd'=16,'row'=2] {'row'}, use_global_device_ids=true, to_apply=%region_5.6 | all-reduce | flops 2 | bytes 16 | tf_op jit(solution)/shard_map/psum | solution.py:85
  81.0 42.2 %all-reduce.3 = (f32[]{:T(128)}, f32[]{:T(128)}) all-reduce(f32[]{:T(128)} %get-tuple-element.9, f32[]{:T(128)} %get-tuple-element.10), channel_id=1, replica_groups=mesh['ccd'=16,'row'=2] {'ccd'}, use_global_device_ids=true, to_apply=%region_6.7 | all-reduce | flops 2 | bytes 16 | tf_op jit(solution)/shard_map/psum | solution.py:85
  126.7 0.8 copy-done.6
  127.5 0.7 convolution_bitcast_fusion
  128.2 0.7 convolution_bitcast_fusion.1
  128.9 0.3 copy-done.7
  129.2 0.7 fusion.15
  129.9 0.8 div.22
  (76 shorter events, 3.6 us)
Async XLA Ops:
  0.6 21.8 %copy-start = (bf16[1,41,41]{2,1,0:T(8,128)(2,1)S(1)}, bf16[1,41,41]{2,1,0:T(8,128)(2,1)}, u32[]{:S(2)}) copy-start(bf16[1,41,41]{2,1,0:T(8,128)(2,1)} %param.20) | copy-start | bytes 10090
  2.5 57.0 %collective-permute-start.1 = (bf16[20,4096]{1,0:T(8,128)(2,1)}, bf16[20,4096]{1,0:T(8,128)(2,1)}, u32[]{:S(2)}, u32[]{:S(2)}) collective-permute-start(bf16[20,4096]{1,0:T(8,128)(2,1)} %get-tuple-element.55), channel_id=1, source_target_pairs={{0,1},{2,3},{4,5},{6,7},{8,9},{10,11},{12,13},{14,15},{16,17},{18,... | collective-permute-start | bytes 491528 | tf_op jit(solution)/shard_map/ppermute | solution.py:21
  5.5 54.0 %collective-permute-start.2 = (bf16[20,4096]{1,0:T(8,128)(2,1)}, bf16[20,4096]{1,0:T(8,128)(2,1)}, u32[]{:S(2)}, u32[]{:S(2)}) collective-permute-start(bf16[20,4096]{1,0:T(8,128)(2,1)} %get-tuple-element.56), channel_id=1, source_target_pairs={{1,0},{3,2},{5,4},{7,6},{9,8},{11,10},{13,12},{15,14},{17,16},{19,... | collective-permute-start | bytes 491528 | tf_op jit(solution)/shard_map/ppermute | solution.py:22
  8.3 43.2 %collective-permute-start = (f32[8,2048]{1,0:T(8,128)}, f32[8,2048]{1,0:T(8,128)}, u32[]{:S(2)}, u32[]{:S(2)}) collective-permute-start(f32[8,2048]{1,0:T(8,128)} %slice_bitcast_fusion.11), channel_id=1, source_target_pairs={{1,0},{3,2},{5,4},{7,6},{9,8},{11,10},{13,12},{15,14},{17,16},{19,... | collective-permute-start | bytes 196616 | tf_op jit(solution)/shard_map/ppermute | solution.py:30
  11.2 0.5 copy-start.12
  13.6 21.5 %all-to-all-start = ((s32[16,2,1]{1,2,0:T(1,128)}), s32[16,2,1]{1,2,0:T(1,128)}, u32[]{:S(2)}, u32[]{:S(2)}) async-start(s32[16,2,1]{1,2,0:T(1,128)} %bitcast.4), calls=%async_computation | async-start | bytes 16384 | tf_op jit(solution)/shard_map/all_to_all | solution.py:136
  24.0 3.0 %copy-start.14 = (bf16[1,24]{1,0:T(2,128)(2,1)S(1)}, bf16[1,24]{1,0:T(2,128)(2,1)}, u32[]{:S(2)}) copy-start(bf16[1,24]{1,0:T(2,128)(2,1)} %param.13) | copy-start | bytes 148
  24.0 4.1 %copy-start.13 = (s32[1,16]{1,0:T(1,128)S(1)}, s32[1,16]{1,0:T(1,128)}, u32[]{:S(2)}) copy-start(s32[1,16]{1,0:T(1,128)} %param.16) | copy-start | bytes 196
  24.0 4.7 %copy-start.10 = (bf16[1,2048]{1,0:T(2,128)(2,1)S(1)}, bf16[1,2048]{1,0:T(2,128)(2,1)}, u32[]{:S(2)}) copy-start(bf16[1,2048]{1,0:T(2,128)(2,1)} %param.15) | copy-start | bytes 12292
  24.0 5.9 %copy-start.11 = (bf16[1,15,15]{2,1,0:T(8,128)(2,1)S(1)}, bf16[1,15,15]{2,1,0:T(8,128)(2,1)}, u32[]{:S(2)}) copy-start(bf16[1,15,15]{2,1,0:T(8,128)(2,1)} %param.21) | copy-start | bytes 1354
  30.6 20.9 %copy-start.8 = (f32[1,24,2048]{2,1,0:T(8,128)S(1)}, f32[1,24,2048]{2,1,0:T(8,128)}, u32[]{:S(2)}) copy-start(f32[1,24,2048]{2,1,0:T(8,128)} %param.11) | copy-start | bytes 589828
  35.2 14.2 %all-to-all-start.1 = ((s32[16,2,1]{1,2,0:T(1,128)}), s32[16,2,1]{1,2,0:T(1,128)S(1)}, u32[]{:S(2)}, u32[]{:S(2)}) async-start(s32[16,2,1]{1,2,0:T(1,128)} %bitcast.401), calls=%async_computation.1 | async-start | bytes 16384 | tf_op jit(solution)/shard_map/all_to_all | solution.py:137
  55.1 15.5 %all-to-all-start.2 = ((bf16[32,24,128]{2,1,0:T(8,128)(2,1)}), bf16[32,24,128]{2,1,0:T(8,128)(2,1)}, u32[]{:S(2)}, u32[]{:S(2)}) async-start(bf16[32,24,128]{2,1,0:T(8,128)(2,1)} %copy.95), calls=%async_computation.2 | async-start | bytes 393216 | tf_op jit(solution)/shard_map/all_to_all | solution.py:135
  63.2 1.0 copy-start.4
  63.4 1.5 %copy-start.3 = (bf16[5,256,128,1]{2,0,1,3:T(8,128)(2,1)S(1)}, bf16[5,256,128,1]{2,0,1,3:T(8,128)(2,1)}, u32[]{:S(2)}) copy-start(bf16[5,256,128,1]{2,0,1,3:T(8,128)(2,1)} %get-tuple-element.13) | copy-start | bytes 983044
  64.9 1.0 copy-start.2
  65.6 1.1 copy-start.1
  69.4 0.9 copy-start.9
  72.7 52.5 %collective-permute-start.3 = (bf16[7,4096]{1,0:T(8,128)(2,1)S(1)}, bf16[7,4096]{1,0:T(8,128)(2,1)S(1)}, u32[]{:S(2)}, u32[]{:S(2)}) collective-permute-start(bf16[7,4096]{1,0:T(8,128)(2,1)S(1)} %get-tuple-element.53), channel_id=1, source_target_pairs={{0,1},{2,3},{4,5},{6,7},{8,9},{10,11},{12,13},{14,15},{16,17},{18,... | collective-permute-start | bytes 172040 | tf_op jit(solution)/shard_map/ppermute | solution.py:21
  75.0 50.1 %collective-permute-start.4 = (bf16[7,4096]{1,0:T(8,128)(2,1)S(1)}, bf16[7,4096]{1,0:T(8,128)(2,1)S(1)}, u32[]{:S(2)}, u32[]{:S(2)}) collective-permute-start(bf16[7,4096]{1,0:T(8,128)(2,1)S(1)} %get-tuple-element.54), channel_id=1, source_target_pairs={{1,0},{3,2},{5,4},{7,6},{9,8},{11,10},{13,12},{15,14},{17,16},{19,... | collective-permute-start | bytes 172040 | tf_op jit(solution)/shard_map/ppermute | solution.py:22
  126.4 1.1 copy-start.6
  126.6 1.6 %copy-start.5 = (bf16[5,256,128,1]{2,0,1,3:T(8,128)(2,1)S(1)}, bf16[5,256,128,1]{2,0,1,3:T(8,128)(2,1)}, u32[]{:S(2)}) copy-start(bf16[5,256,128,1]{2,0,1,3:T(8,128)(2,1)} %get-tuple-element.21) | copy-start | bytes 983044
  128.2 1.0 copy-start.7
